TPU v7x, 32 devices: a whole 2x2x4 slice. The times are simulated.
32 devices in a mesh: dp: 8 (over z, x), mp: 4 (over y, core).
Axes of the slice: x: 2, y: 2, z: 4, core: 2. Of those that a mesh axis runs over, the one named last changes fastest.
Arguments:
- gating_logits: bfloat16 [8, 3, 64, 7168], P('dp', None, None, 'mp'), may hold values from -6 to 6
- lifted_hidden_values: bfloat16 [8, 3, 64, 7168], P('dp', None, None, 'mp'), may hold values from -6 to 6
- loss_output_grad: bfloat16 [8, 3, 64, 2048], P('dp', None, None, 'mp'), may hold values from -160 to 160
- arrival_flags: int32 [8], P('dp'), may hold values from 0 to 1, as said below
- block_owner_map: int32 [8, 3], P('dp'), may hold values from 0 to 7, as said below
- decoder_multipliers: int32 [8, 3], P('dp'), may hold values from 1 to 4
- block_piece_number: int32 [8], replicated, may hold values from 1 to 2, as said below
Outputs:
- down_grad: float32 [2048, 7168], P('dp', 'mp')
Inputs may be any that keep to these rules, and one draw needn't show every extreme that they name: `arrival_flags`: at least one replica survives. `block_owner_map`: row i lists the partitions (i + r + k) mod 8 for k < 3, with one r for all rows. `block_piece_number`: some partition has exactly 2 live tiles.
All inputs are finite; a program needn't handle non-finite values.
Results may differ from a plain program's by a relative error of at most 0.0042.
Values may be sent and summed in bfloat16 or wider, within the bound.
No kernel may reach another device: no remote copies, remote signals or barrier semaphores. Data moves between devices by JAX's collectives and lax.ppermute only.
A program may use at most 128 MiB of HBM per device.

v0:
```python
import jax
import jax.numpy as jnp
from jax import lax
from jax.sharding import PartitionSpec as P

TILE = 32


def slot_product(columns, hidden_k):
    return lax.dot_general(
        columns, hidden_k, (((0,), (0,)), ((), ())), preferred_element_type=jnp.float32
    )


def on_device(
    gating_logits,
    lifted_hidden_values,
    loss_output_grad,
    arrival_flags,
    block_owner_map,
    decoder_multipliers,
    block_piece_number,
):
    slot_tally = gating_logits.shape[1]
    tok_rows = gating_logits.shape[2]
    part_ids = jnp.arange(block_piece_number.shape[0], dtype=jnp.int32)
    slot_tiles = jnp.sum(
        jnp.where(block_owner_map[0][:, None] == part_ids[None, :], block_piece_number[None, :], 0),
        axis=1,
    )
    live_rows = slot_tiles * TILE
    live_mask = jnp.arange(tok_rows, dtype=jnp.int32)[None, :] < live_rows[:, None]
    hidden = (
        jax.nn.silu(gating_logits[0].astype(jnp.float32))
        * lifted_hidden_values[0].astype(jnp.float32)
        * live_mask[:, :, None].astype(jnp.float32)
    ).astype(jnp.bfloat16)
    down_kernel_array = arrival_flags[0].astype(jnp.float32) * decoder_multipliers[0].astype(
        jnp.float32
    )
    token_sum = jnp.sum(down_kernel_array * live_rows.astype(jnp.float32))
    cotangent = lax.all_gather(loss_output_grad, "mp", axis=3, tiled=True)[0]
    feature_total = cotangent.shape[2]
    block_count = 8
    block_rows = feature_total // block_count

    def project(carry, block_num):
        columns = lax.dynamic_slice_in_dim(cotangent, block_num * block_rows, block_rows, 2)
        running_total = jnp.zeros((block_rows, hidden.shape[2]), jnp.float32)
        for slot_num in range(slot_tally):
            product = slot_product(columns[slot_num], hidden[slot_num])
            running_total = running_total + down_kernel_array[slot_num] * product
        return (carry, running_total)

    _, blocks = lax.scan(
        project, jnp.zeros((), jnp.float32), jnp.arange(block_count, dtype=jnp.int32)
    )
    gradient = blocks.reshape(feature_total, hidden.shape[2])
    replicas = lax.axis_size("dp")
    stacked = gradient.reshape(replicas, feature_total // replicas, hidden.shape[2])
    received = lax.all_to_all(stacked, "dp", split_axis=0, concat_axis=0, tiled=True)
    total_tokens = lax.psum(token_sum, "dp")
    return jnp.sum(received, axis=0) / total_tokens


def solution(mesh):
    return jax.shard_map(
        on_device,
        mesh=mesh,
        in_specs=(
            P("dp", None, None, "mp"),
            P("dp", None, None, "mp"),
            P("dp", None, None, "mp"),
            P("dp"),
            P("dp", None),
            P("dp", None),
            P(),
        ),
        out_specs=P("dp", "mp"),
        check_vma=False,
    )
```

profile of v0, /device:TPU:8, one launch (start us, length us, event | category | flops | bytes accessed | tf_op | source)
XLA Modules:
  0.0 428.0 jit_solution(8810284644568872122)
XLA Ops:
  1.6 8.8 %all_gather.3 = bf16[1,3,64,2048]{3,2,1,0:T(8,128)(2,1)S(1)} all-gather(bf16[1,3,64,512]{3,2,1,0:T(8,128)(2,1)} %param.11), channel_id=1, replica_groups=mesh['dp'=8,'mp'=4] {'mp'}, dimensions={3}, use_global_device_ids=true | all-gather | bytes 983040 | tf_op jit(solution)/shard_map/all_gather | solution.py:42
  10.4 1.3 multiply_reduce_fusion
  11.7 1.8 fusion.18
  13.5 73.1 %while.10 = (s32[]{:T(128)}, f32[8,256,1792]{2,1,0:T(8,128)}, f32[3]{0:T(128)S(1)}, s32[8]{0:T(128)S(1)}, bf16[3,64,2048]{2,1,0:T(8,128)(2,1)S(1)}, /*index=5*/b...) while((s32[]{:T(128)}, f32[8,256,1792]{2,1,0:T(8,128)}, ...), condition=%wide.region_2.3_spmd, body=%wide.region_1.2_spmd.sunk | while | flops 178454528 | bytes 9962747 | solution.py:55
  15.5 2.3 convolution_multiply_fusion.4
  17.8 2.5 fusion.31
  20.4 2.3 fusion.32
  24.6 2.3 convolution_multiply_fusion.4
  26.9 2.6 fusion.31
  29.5 2.3 fusion.32
  33.7 2.3 convolution_multiply_fusion.4
  36.0 2.5 fusion.31
  38.6 2.3 fusion.32
  42.8 2.3 convolution_multiply_fusion.4
  45.2 2.6 fusion.31
  47.7 2.4 fusion.32
  52.0 2.3 convolution_multiply_fusion.4
  54.3 2.5 fusion.31
  56.9 2.4 fusion.32
  61.2 2.3 convolution_multiply_fusion.4
  63.5 2.5 fusion.31
  66.1 2.3 fusion.32
  70.3 2.3 convolution_multiply_fusion.4
  72.6 2.6 fusion.31
  75.2 2.3 fusion.32
  79.4 2.3 convolution_multiply_fusion.4
  81.8 2.6 fusion.31
  84.3 2.3 fusion.32
  86.7 6.3 %all-to-all-start = ((f32[8,256,1792]{2,1,0:T(8,128)}), f32[8,256,1792]{2,1,0:T(8,128)}, u32[]{:S(2)}, u32[]{:S(2)}) async-start(f32[8,256,1792]{2,1,0:T(8,128)} %get-tuple-element.37), calls=%async_computation | async-start | bytes 29360128 | tf_op jit(solution)/shard_map/all_to_all | solution.py:61
  92.9 326.8 %psum.7 = f32[]{:T(128)} all-reduce(f32[]{:T(128)} %get-tuple-element.50), channel_id=1, replica_groups=mesh['dp'=8,'mp'=4] {'dp'}, use_global_device_ids=true, to_apply=%region_5.6 | all-reduce | flops 1 | bytes 8 | tf_op jit(solution)/shard_map/psum | solution.py:62
  419.7 6.3 %reduce_sum.28 = f32[256,1792]{1,0:T(8,128)S(1)} reduce(f32[8,256,1792]{2,1,0:T(8,128)} %all-to-all-done, f32[]{:T(128)} %constant.7.clone.1), dimensions={0}, to_apply=%region_3.4 | reduce | flops 3211264 | bytes 16515076 | tf_op jit(solution)/shard_map/reduce_sum | solution.py:63
  426.0 2.0 broadcast_divide_fusion
  (22 shorter events, 11.0 us)
Async XLA Ops:
  86.7 333.1 %all-to-all-start = ((f32[8,256,1792]{2,1,0:T(8,128)}), f32[8,256,1792]{2,1,0:T(8,128)}, u32[]{:S(2)}, u32[]{:S(2)}) async-start(f32[8,256,1792]{2,1,0:T(8,128)} %get-tuple-element.37), calls=%async_computation | async-start | bytes 29360128 | tf_op jit(solution)/shard_map/all_to_all | solution.py:61
where the time goes:
time: 429 us; the launch traced here: 428 us
  blocking collectives  336 us (78%)
  matrix products  57.8 us (13%)
  other arithmetic  12.3 us (3%)
  local copies, waits for them, and re-layouts  10 us (2%)
  starting transfers between devices  6.25 us (1%)
  loops' own time  5.34 us (1%)
    psum x1, blocking collectives, on_device(): total_tokens = lax.psum(token_sum, 'dp')  327 us
    dot_general x24, matrix products, slot_product(): lax.dot_general(columns, hidden_k, (((0,), (0,)), ((), ())), preferred_el...  57.8 us
    all_gather x1, blocking collectives, on_device(): cotangent = lax.all_gather(loss_output_grad, 'mp', axis=3, tiled=True)[0]  8.82 us
  transfers between devices with their start and end apart: 1, of which 0 were waited for; matrix products, arithmetic and copies ran while one was open for 0% of the time, Pallas kernels for 0%

commit v1 on v0

v1 whole, which is shorter than its diff:
```python
import jax
import jax.numpy as jnp
from jax import lax
from jax.sharding import PartitionSpec as P

TILE = 32
CHUNKS = 2


def project(cots, hs):
    return lax.dot_general(cots, hs, (((0,), (0,)), ((), ())), preferred_element_type=jnp.float32)


def on_device(gate, up, cot, flags, owner, mult, pieces):
    _, slots, tok, cols = gate.shape
    feats = cot.shape[3]
    dp = lax.axis_size("dp")
    mp = lax.axis_size("mp")
    outer, inner = mp, dp // mp
    i = lax.axis_index("dp")
    z = i // inner
    x = i % inner
    ids = jnp.arange(pieces.shape[0], dtype=jnp.int32)
    tiles = jnp.sum(jnp.where(owner[0][:, None] == ids[None, :], pieces[None, :], 0), axis=1)
    live = tiles * TILE
    weight = flags[0].astype(jnp.float32) * mult[0].astype(jnp.float32)
    tokens = jnp.sum(weight * live.astype(jnp.float32))
    rows = slots * tok
    block = feats // inner
    scaled = (cot[0].astype(jnp.float32) * weight[:, None, None]).astype(jnp.bfloat16).reshape(rows, feats)
    if inner == 2:
        swapped = jnp.concatenate([scaled[:, block:], scaled[:, :block]], axis=1)
        scaled = jnp.where(x == 0, scaled, swapped)
    both = ("dp", "mp")
    perm = []
    for a in range(outer):
        for b in range(inner):
            for m in range(mp):
                perm.append(((a * inner + b) * mp + m, (m * inner + b) * mp + (a ^ m)))
    moved = lax.ppermute(scaled, both, perm)
    cots = lax.all_gather(moved, "mp", axis=0, tiled=True)
    total = lax.psum(tokens, "dp")

    def perm_z(pairs):
        return [(a * inner + b, c * inner + b) for a, c in pairs for b in range(inner)]

    sizes = [cols // CHUNKS] * CHUNKS
    lo = 0
    mask = (jnp.arange(tok, dtype=jnp.int32)[None, :] < live[:, None])
    outs = []
    for c, w in enumerate(sizes):
        g = gate[0, :, :, lo : lo + w].astype(jnp.float32)
        u = up[0, :, :, lo : lo + w].astype(jnp.float32)
        lo += w
        h = (jax.nn.silu(g) * u * mask[:, :, None].astype(jnp.float32)).astype(jnp.bfloat16).reshape(rows, w)
        ha = lax.ppermute(h, "dp", perm_z([(0, 1), (1, 0), (2, 3), (3, 2)]))
        hq = lax.ppermute(h, "dp", perm_z([(0, 2), (2, 0), (1, 3), (3, 1)]))
        hf1 = lax.ppermute(h, "dp", perm_z([(1, 2), (2, 1)]))
        hf2 = lax.ppermute(hq, "dp", perm_z([(1, 0), (2, 3)]))
        hf = jnp.where((z == 1) | (z == 2), hf1, hf2)
        hs = jnp.concatenate([h, ha, hq, hf], axis=0)
        if inner == 2:
            send = project(cots[:, block:], hs).astype(jnp.bfloat16)
            got = lax.ppermute(send, "dp", [(d, d ^ 1) for d in range(dp)])
            outs.append((project(cots[:, :block], hs) + got.astype(jnp.float32)) / total)
        else:
            partial = project(cots, hs).astype(jnp.bfloat16).reshape(inner, block, w)
            groups = [[a * inner + b for b in range(inner)] for a in range(outer)]
            got = lax.all_to_all(partial, "dp", 0, 0, axis_index_groups=groups, tiled=True)
            outs.append(jnp.sum(got.astype(jnp.float32), axis=0) / total)
    return jnp.concatenate(outs, axis=1)


def solution(mesh):
    return jax.shard_map(
        on_device,
        mesh=mesh,
        in_specs=(
            P("dp", None, None, "mp"),
            P("dp", None, None, "mp"),
            P("dp", None, None, "mp"),
            P("dp"),
            P("dp", None),
            P("dp", None),
            P(),
        ),
        out_specs=P("dp", "mp"),
        check_vma=False,
    )
```

time: 429 us -> 110 us (0.26)
  the two profiles are of different devices: /device:TPU:8 before, /device:TPU:4 now
where the time goes in v1:
time: 110 us; the launch traced here: 109 us
  waiting for transfers between devices  35.7 us (32%)
  blocking collectives  34.6 us (31%)
  starting transfers between devices  24 us (22%)
  matrix products  8.79 us (8%)
  other arithmetic  3.76 us (3%)
  local copies, waits for them, and re-layouts  1.72 us (2%)
    psum x1, blocking collectives, on_device(): total = lax.psum(tokens, 'dp')  27.1 us
    ppermute x2, waiting for transfers between devices, on_device(): hq = lax.ppermute(h, 'dp', perm_z([(0, 2), (2, 0), (1, 3), (3, 1)]))  15.4 us
    ppermute x2, waiting for transfers between devices, on_device(): hf2 = lax.ppermute(hq, 'dp', perm_z([(1, 0), (2, 3)]))  11.1 us
    dot_general x4, matrix products, project(): lax.dot_general(cots, hs, (((0,), (0,)), ((), ())), preferred_element_typ...  8.79 us
    ppermute x2, starting transfers between devices, on_device(): ha = lax.ppermute(h, 'dp', perm_z([(0, 1), (1, 0), (2, 3), (3, 2)]))  8.11 us
    all_gather x1, blocking collectives, on_device(): cots = lax.all_gather(moved, 'mp', axis=0, tiled=True)  7.47 us
    ppermute x2, starting transfers between devices, on_device(): hq = lax.ppermute(h, 'dp', perm_z([(0, 2), (2, 0), (1, 3), (3, 1)]))  6.66 us
    ppermute x2, waiting for transfers between devices, on_device(): ha = lax.ppermute(h, 'dp', perm_z([(0, 1), (1, 0), (2, 3), (3, 2)]))  6.41 us
  transfers between devices with their start and end apart: 11, of which 4 were waited for; matrix products, arithmetic and copies ran while one was open for 7% of the time, Pallas kernels for 0%

profile of v1, /device:TPU:4, one launch (start us, length us, event | category | flops | bytes accessed | tf_op | source)
XLA Modules:
  0.0 109.4 jit_solution(2149252115974620749)
XLA Ops:
  0.0 0.9 select_reduce_fusion
  0.9 0.1 fusion.19
  0.9 0.1 reshape.63
  1.0 1.4 %fusion.24 = (bf16[1,3,64,896]{3,2,1,0:T(8,128)(2,1)S(1)}, bf16[1,3,64,896]{3,2,1,0:T(8,128)(2,1)S(1)}, bf16[1,3,64,896]{3,2,1,0:T(8,128)(2,1)S(1)}, bf16[1,3,64,896]{3,2,1,0:T(8,128)(2,1)S(1)}) fusion(bf16[1,3,64,1792]{3,2,1,0:T(8,128)(2,1)} %param.7, bf16[1,3,64,1792]{3,2,1,0:T(8,128)(2,1)} %param.8), kind=kLoop, calls=%fused_computation.45 | loop fusion | bytes 2752512 | tf_op jit(solution)/shard_map/slice | solution.py:52
  2.5 0.6 fusion.13
  3.1 2.7 %collective-permute-start.2 = (bf16[192,896]{1,0:T(8,128)(2,1)S(1)}, bf16[192,896]{1,0:T(8,128)(2,1)S(1)}, u32[]{:S(2)}, u32[]{:S(2)}) collective-permute-start(bf16[192,896]{1,0:T(8,128)(2,1)S(1)} %get-tuple-element.13), channel_id=1, source_target_pairs={{0,16},{4,20},{16,0},{20,4},{8,24},{12,28},{24,8},{28,12},{1,17},{... | collective-permute-start | bytes 1032200 | tf_op jit(solution)/shard_map/ppermute | solution.py:57
  6.4 0.6 multiply_reduce_fusion
  7.0 0.1 mul.72
  7.0 0.1 mul.73
  7.1 0.1 fusion.14
  7.2 0.1 maximum_select_fusion
  7.4 2.2 %collective-permute-start = (bf16[192,512]{1,0:T(8,128)(2,1)S(1)}, bf16[192,512]{1,0:T(8,128)(2,1)S(1)}, u32[]{:S(2)}, u32[]{:S(2)}) collective-permute-start(bf16[192,512]{1,0:T(8,128)(2,1)S(1)} %maximum_select_fusion), channel_id=1, source_target_pairs={{0,0},{1,9},{2,18},{3,27},{4,4},{5,13},{6,22},{7,31},{8,1},{9,8},{... | collective-permute-start | bytes 589832 | tf_op jit(solution)/shard_map/ppermute | solution.py:40
  9.6 0.7 collective-permute-start.3
  10.3 4.0 %collective-permute-start.7 = (bf16[192,896]{1,0:T(8,128)(2,1)S(1)}, bf16[192,896]{1,0:T(8,128)(2,1)}, u32[]{:S(2)}, u32[]{:S(2)}) collective-permute-start(bf16[192,896]{1,0:T(8,128)(2,1)S(1)} %get-tuple-element.14), channel_id=1, source_target_pairs={{0,16},{4,20},{16,0},{20,4},{8,24},{12,28},{24,8},{28,12},{1,17},{... | collective-permute-start | bytes 1032200 | tf_op jit(solution)/shard_map/ppermute | solution.py:57
  14.3 15.4 %collective-permute-done.2 = bf16[192,896]{1,0:T(8,128)(2,1)S(1)} collective-permute-done((bf16[192,896]{1,0:T(8,128)(2,1)S(1)}, bf16[192,896]{1,0:T(8,128)(2,1)S(1)}, u32[]{:S(2)}, u32[]{:S(2)}) %collective-permute-start.2) | collective-permute-done | bytes 344096 | tf_op jit(solution)/shard_map/ppermute | solution.py:57
  29.7 1.3 %collective-permute-start.4 = (bf16[192,896]{1,0:T(8,128)(2,1)S(1)}, bf16[192,896]{1,0:T(8,128)(2,1)S(1)}, u32[]{:S(2)}, u32[]{:S(2)}) collective-permute-start(bf16[192,896]{1,0:T(8,128)(2,1)S(1)} %collective-permute-done.2), channel_id=1, source_target_pairs={{8,0},{12,4},{16,24},{20,28},{9,1},{13,5},{17,25},{21,29},{10,2},{... | collective-permute-start | bytes 1032200 | tf_op jit(solution)/shard_map/ppermute | solution.py:59
  31.0 4.0 %collective-permute-start.1 = (bf16[192,896]{1,0:T(8,128)(2,1)S(1)}, bf16[192,896]{1,0:T(8,128)(2,1)}, u32[]{:S(2)}, u32[]{:S(2)}) collective-permute-start(bf16[192,896]{1,0:T(8,128)(2,1)S(1)} %get-tuple-element.13), channel_id=1, source_target_pairs={{0,8},{4,12},{8,0},{12,4},{16,24},{20,28},{24,16},{28,20},{1,9},{5... | collective-permute-start | bytes 1032200 | tf_op jit(solution)/shard_map/ppermute | solution.py:56
  34.9 2.8 %collective-permute-done = bf16[192,512]{1,0:T(8,128)(2,1)S(1)} collective-permute-done((bf16[192,512]{1,0:T(8,128)(2,1)S(1)}, bf16[192,512]{1,0:T(8,128)(2,1)S(1)}, u32[]{:S(2)}, u32[]{:S(2)}) %collective-permute-start) | collective-permute-done | bytes 196640 | tf_op jit(solution)/shard_map/ppermute | solution.py:40
  37.8 0.7 collective-permute-start.8
  38.4 7.5 %all_gather.3 = bf16[768,512]{1,0:T(8,128)(2,1)S(1)} all-gather(bf16[192,512]{1,0:T(8,128)(2,1)S(1)} %collective-permute-done), channel_id=1, replica_groups=mesh['dp'=8,'mp'=4] {'mp'}, dimensions={0}, use_global_device_ids=true | all-gather | bytes 983040 | tf_op jit(solution)/shard_map/all_gather | solution.py:41
  45.9 4.2 %collective-permute-start.6 = (bf16[192,896]{1,0:T(8,128)(2,1)S(1)}, bf16[192,896]{1,0:T(8,128)(2,1)S(1)}, u32[]{:S(2)}, u32[]{:S(2)}) collective-permute-start(bf16[192,896]{1,0:T(8,128)(2,1)S(1)} %get-tuple-element.14), channel_id=1, source_target_pairs={{0,8},{4,12},{8,0},{12,4},{16,24},{20,28},{24,16},{28,20},{1,9},{5... | collective-permute-start | bytes 1032200 | tf_op jit(solution)/shard_map/ppermute | solution.py:56
  50.1 1.3 %collective-permute-start.9 = (bf16[192,896]{1,0:T(8,128)(2,1)}, bf16[192,896]{1,0:T(8,128)(2,1)S(1)}, u32[]{:S(2)}, u32[]{:S(2)}) collective-permute-start(bf16[192,896]{1,0:T(8,128)(2,1)} %collective-permute-done.7), channel_id=1, source_target_pairs={{8,0},{12,4},{16,24},{20,28},{9,1},{13,5},{17,25},{21,29},{10,2},{... | collective-permute-start | bytes 1032200 | tf_op jit(solution)/shard_map/ppermute | solution.py:59
  51.4 6.4 %collective-permute-done.1 = bf16[192,896]{1,0:T(8,128)(2,1)} collective-permute-done((bf16[192,896]{1,0:T(8,128)(2,1)S(1)}, bf16[192,896]{1,0:T(8,128)(2,1)}, u32[]{:S(2)}, u32[]{:S(2)}) %collective-permute-start.1) | collective-permute-done | bytes 344096 | tf_op jit(solution)/shard_map/ppermute | solution.py:56
  57.8 1.6 %convolution_convert_fusion.1 = bf16[256,896]{1,0:T(8,128)(2,1)S(1)} fusion(bf16[768,512]{1,0:T(8,128)(2,1)S(1)} %all_gather.3, bf16[192,896]{1,0:T(8,128)(2,1)S(1)} %broadcast_select_fusion.1, bf16[192,896]{1,0:T(8,128)(2,1)S(1)} %collective-permute-done.2, bf16[192,896]{1,0:T(8,128)(2,1)} %collective-permute-done.1, bf16[192,896]{1,0:T(8,128)(2,1)S(1)} %get-tuple-element.13), kind=kOutput, calls=%fused_computation.8 | convolution fusion | flops 358055936 | bytes 2228224 | tf_op jit(solution)/shard_map/dot_general | solution.py:11
  59.4 1.6 %collective-permute-start.5 = (bf16[256,896]{1,0:T(8,128)(2,1)S(1)}, bf16[256,896]{1,0:T(8,128)(2,1)S(1)}, u32[]{:S(2)}, u32[]{:S(2)}) collective-permute-start(bf16[256,896]{1,0:T(8,128)(2,1)S(1)} %convolution_convert_fusion.1), channel_id=1, source_target_pairs={{0,4},{4,0},{8,12},{12,8},{16,20},{20,16},{24,28},{28,24},{1,5},{5... | collective-permute-start | bytes 1376264 | tf_op jit(solution)/shard_map/ppermute | solution.py:64
  61.0 11.1 %collective-permute-done.9 = bf16[192,896]{1,0:T(8,128)(2,1)S(1)} collective-permute-done((bf16[192,896]{1,0:T(8,128)(2,1)}, bf16[192,896]{1,0:T(8,128)(2,1)S(1)}, u32[]{:S(2)}, u32[]{:S(2)}) %collective-permute-start.9) | collective-permute-done | bytes 344096 | tf_op jit(solution)/shard_map/ppermute | solution.py:59
  72.2 2.5 %convolution_convert_fusion = bf16[256,896]{1,0:T(8,128)(2,1)} fusion(bf16[768,512]{1,0:T(8,128)(2,1)S(1)} %all_gather.3, bf16[192,896]{1,0:T(8,128)(2,1)S(1)} %broadcast_select_fusion, bf16[192,896]{1,0:T(8,128)(2,1)} %collective-permute-done.7, bf16[192,896]{1,0:T(8,128)(2,1)S(1)} %collective-permute-done.6, bf16[192,896]{1,0:T(8,128)(2,1)S(1)} %get-tuple-element.14), kind=kOutput, calls=%fused_computation.7 | convolution fusion | flops 358055936 | bytes 2228224 | tf_op jit(solution)/shard_map/dot_general | solution.py:11
  74.7 1.5 %collective-permute-start.10 = (bf16[256,896]{1,0:T(8,128)(2,1)}, bf16[256,896]{1,0:T(8,128)(2,1)}, u32[]{:S(2)}, u32[]{:S(2)}) collective-permute-start(bf16[256,896]{1,0:T(8,128)(2,1)} %convolution_convert_fusion), channel_id=1, source_target_pairs={{0,4},{4,0},{8,12},{12,8},{16,20},{20,16},{24,28},{28,24},{1,5},{5... | collective-permute-start | bytes 1376264 | tf_op jit(solution)/shard_map/ppermute | solution.py:64
  76.2 27.1 %psum.7 = f32[]{:T(128)} all-reduce(f32[]{:T(128)} %get-tuple-element.5), channel_id=1, replica_groups=mesh['dp'=8,'mp'=4] {'dp'}, use_global_device_ids=true, to_apply=%region_2.3 | all-reduce | flops 1 | bytes 8 | tf_op jit(solution)/shard_map/psum | solution.py:42
  103.3 2.3 %fusion.1 = f32[256,896]{1,0:T(8,128)S(1)} fusion(bf16[256,896]{1,0:T(8,128)(2,1)S(1)} %collective-permute-done.5, f32[]{:T(128)} %psum.7, bf16[768,512]{1,0:T(8,128)(2,1)S(1)} %all_gather.3, bf16[192,896]{1,0:T(8,128)(2,1)S(1)} %broadcast_select_fusion.1, bf16[192,896]{1,0:T(8,128)(2,1)S(1)} %copy-done.3, bf16[192,896]{1,0:T(8,128)(2,1)} %collective-permute-done.1, ...), kind=kOutput, calls=%fused_computation.6 | convolution fusion | flops 358514688 | bytes 3145732 | tf_op jit(solution)/shard_map/dot_general | solution.py:11
  105.6 2.4 %fusion = f32[256,896]{1,0:T(8,128)S(1)} fusion(bf16[256,896]{1,0:T(8,128)(2,1)} %collective-permute-done.10, f32[]{:T(128)} %psum.7, bf16[768,512]{1,0:T(8,128)(2,1)S(1)} %all_gather.3, bf16[192,896]{1,0:T(8,128)(2,1)S(1)} %broadcast_select_fusion, bf16[192,896]{1,0:T(8,128)(2,1)} %collective-permute-done.7, bf16[192,896]{1,0:T(8,128)(2,1)S(1)} %copy-done.5, ...), kind=kOutput, calls=%fused_computation.4 | convolution fusion | flops 358514688 | bytes 3145732 | tf_op jit(solution)/shard_map/dot_general | solution.py:11
  108.0 1.4 %pad_maximum_fusion = f32[256,1792]{1,0:T(8,128)} fusion(f32[256,896]{1,0:T(8,128)S(1)} %fusion, f32[256,896]{1,0:T(8,128)S(1)} %fusion.1), kind=kLoop, calls=%fused_computation | loop fusion | flops 458752 | bytes 3670016 | tf_op jit(solution)/shard_map/concatenate | solution.py:71
  (23 shorter events, 0.1 us)
Async XLA Ops:
  1.0 5.4 %copy-start.1 = (s32[1,3]{1,0:T(1,128)S(1)}, s32[1,3]{1,0:T(1,128)}, u32[]{:S(2)}) copy-start(s32[1,3]{1,0:T(1,128)} %param.12) | copy-start | bytes 40
  1.0 6.1 %copy-start = (bf16[1,3,64,512]{3,2,1,0:T(8,128)(2,1)S(1)}, bf16[1,3,64,512]{3,2,1,0:T(8,128)(2,1)}, u32[]{:S(2)}) copy-start(bf16[1,3,64,512]{3,2,1,0:T(8,128)(2,1)} %param.9) | copy-start | bytes 589828
  3.1 26.6 %collective-permute-start.2 = (bf16[192,896]{1,0:T(8,128)(2,1)S(1)}, bf16[192,896]{1,0:T(8,128)(2,1)S(1)}, u32[]{:S(2)}, u32[]{:S(2)}) collective-permute-start(bf16[192,896]{1,0:T(8,128)(2,1)S(1)} %get-tuple-element.13), channel_id=1, source_target_pairs={{0,16},{4,20},{16,0},{20,4},{8,24},{12,28},{24,8},{28,12},{1,17},{... | collective-permute-start | bytes 1032200 | tf_op jit(solution)/shard_map/ppermute | solution.py:57
  7.4 30.4 %collective-permute-start = (bf16[192,512]{1,0:T(8,128)(2,1)S(1)}, bf16[192,512]{1,0:T(8,128)(2,1)S(1)}, u32[]{:S(2)}, u32[]{:S(2)}) collective-permute-start(bf16[192,512]{1,0:T(8,128)(2,1)S(1)} %maximum_select_fusion), channel_id=1, source_target_pairs={{0,0},{1,9},{2,18},{3,27},{4,4},{5,13},{6,22},{7,31},{8,1},{9,8},{... | collective-permute-start | bytes 589832 | tf_op jit(solution)/shard_map/ppermute | solution.py:40
  9.6 36.3 %collective-permute-start.3 = (bf16[192,896]{1,0:T(8,128)(2,1)S(1)}, bf16[192,896]{1,0:T(8,128)(2,1)S(1)}, u32[]{:S(2)}, u32[]{:S(2)}) collective-permute-start(bf16[192,896]{1,0:T(8,128)(2,1)S(1)} %get-tuple-element.13), channel_id=1, source_target_pairs={{8,16},{12,20},{16,8},{20,12},{9,17},{13,21},{17,9},{21,13},{10,18... | collective-permute-start | bytes 1032200 | tf_op jit(solution)/shard_map/ppermute | solution.py:58
  10.3 39.7 %collective-permute-start.7 = (bf16[192,896]{1,0:T(8,128)(2,1)S(1)}, bf16[192,896]{1,0:T(8,128)(2,1)}, u32[]{:S(2)}, u32[]{:S(2)}) collective-permute-start(bf16[192,896]{1,0:T(8,128)(2,1)S(1)} %get-tuple-element.14), channel_id=1, source_target_pairs={{0,16},{4,20},{16,0},{20,4},{8,24},{12,28},{24,8},{28,12},{1,17},{... | collective-permute-start | bytes 1032200 | tf_op jit(solution)/shard_map/ppermute | solution.py:57
  29.7 28.1 %copy-start.2 = (bf16[192,896]{1,0:T(8,128)(2,1)}, bf16[192,896]{1,0:T(8,128)(2,1)S(1)}, u32[]{:S(2)}) copy-start(bf16[192,896]{1,0:T(8,128)(2,1)S(1)} %collective-permute-done.2) | copy-start | bytes 1032196
  29.7 21.7 %collective-permute-start.4 = (bf16[192,896]{1,0:T(8,128)(2,1)S(1)}, bf16[192,896]{1,0:T(8,128)(2,1)S(1)}, u32[]{:S(2)}, u32[]{:S(2)}) collective-permute-start(bf16[192,896]{1,0:T(8,128)(2,1)S(1)} %collective-permute-done.2), channel_id=1, source_target_pairs={{8,0},{12,4},{16,24},{20,28},{9,1},{13,5},{17,25},{21,29},{10,2},{... | collective-permute-start | bytes 1032200 | tf_op jit(solution)/shard_map/ppermute | solution.py:59
  31.0 26.8 %collective-permute-start.1 = (bf16[192,896]{1,0:T(8,128)(2,1)S(1)}, bf16[192,896]{1,0:T(8,128)(2,1)}, u32[]{:S(2)}, u32[]{:S(2)}) collective-permute-start(bf16[192,896]{1,0:T(8,128)(2,1)S(1)} %get-tuple-element.13), channel_id=1, source_target_pairs={{0,8},{4,12},{8,0},{12,4},{16,24},{20,28},{24,16},{28,20},{1,9},{5... | collective-permute-start | bytes 1032200 | tf_op jit(solution)/shard_map/ppermute | solution.py:56
  37.8 23.2 %collective-permute-start.8 = (bf16[192,896]{1,0:T(8,128)(2,1)S(1)}, bf16[192,896]{1,0:T(8,128)(2,1)S(1)}, u32[]{:S(2)}, u32[]{:S(2)}) collective-permute-start(bf16[192,896]{1,0:T(8,128)(2,1)S(1)} %get-tuple-element.14), channel_id=1, source_target_pairs={{8,16},{12,20},{16,8},{20,12},{9,17},{13,21},{17,9},{21,13},{10,18... | collective-permute-start | bytes 1032200 | tf_op jit(solution)/shard_map/ppermute | solution.py:58
  45.9 26.2 %collective-permute-start.6 = (bf16[192,896]{1,0:T(8,128)(2,1)S(1)}, bf16[192,896]{1,0:T(8,128)(2,1)S(1)}, u32[]{:S(2)}, u32[]{:S(2)}) collective-permute-start(bf16[192,896]{1,0:T(8,128)(2,1)S(1)} %get-tuple-element.14), channel_id=1, source_target_pairs={{0,8},{4,12},{8,0},{12,4},{16,24},{20,28},{24,16},{28,20},{1,9},{5... | collective-permute-start | bytes 1032200 | tf_op jit(solution)/shard_map/ppermute | solution.py:56
  50.1 22.0 %collective-permute-start.9 = (bf16[192,896]{1,0:T(8,128)(2,1)}, bf16[192,896]{1,0:T(8,128)(2,1)S(1)}, u32[]{:S(2)}, u32[]{:S(2)}) collective-permute-start(bf16[192,896]{1,0:T(8,128)(2,1)} %collective-permute-done.7), channel_id=1, source_target_pairs={{8,0},{12,4},{16,24},{20,28},{9,1},{13,5},{17,25},{21,29},{10,2},{... | collective-permute-start | bytes 1032200 | tf_op jit(solution)/shard_map/ppermute | solution.py:59
  59.4 43.9 %collective-permute-start.5 = (bf16[256,896]{1,0:T(8,128)(2,1)S(1)}, bf16[256,896]{1,0:T(8,128)(2,1)S(1)}, u32[]{:S(2)}, u32[]{:S(2)}) collective-permute-start(bf16[256,896]{1,0:T(8,128)(2,1)S(1)} %convolution_convert_fusion.1), channel_id=1, source_target_pairs={{0,4},{4,0},{8,12},{12,8},{16,20},{20,16},{24,28},{28,24},{1,5},{5... | collective-permute-start | bytes 1376264 | tf_op jit(solution)/shard_map/ppermute | solution.py:64
  72.1 31.1 %copy-start.3 = (bf16[192,896]{1,0:T(8,128)(2,1)S(1)}, bf16[192,896]{1,0:T(8,128)(2,1)}, u32[]{:S(2)}) copy-start(bf16[192,896]{1,0:T(8,128)(2,1)} %copy-done.2) | copy-start | bytes 1032196
  72.2 2.5 %copy-start.4 = (bf16[192,896]{1,0:T(8,128)(2,1)}, bf16[192,896]{1,0:T(8,128)(2,1)S(1)}, u32[]{:S(2)}) copy-start(bf16[192,896]{1,0:T(8,128)(2,1)S(1)} %collective-permute-done.6) | copy-start | bytes 1032196
  74.7 30.9 %collective-permute-start.10 = (bf16[256,896]{1,0:T(8,128)(2,1)}, bf16[256,896]{1,0:T(8,128)(2,1)}, u32[]{:S(2)}, u32[]{:S(2)}) collective-permute-start(bf16[256,896]{1,0:T(8,128)(2,1)} %convolution_convert_fusion), channel_id=1, source_target_pairs={{0,4},{4,0},{8,12},{12,8},{16,20},{20,16},{24,28},{28,24},{1,5},{5... | collective-permute-start | bytes 1376264 | tf_op jit(solution)/shard_map/ppermute | solution.py:64
  103.3 2.3 %copy-start.5 = (bf16[192,896]{1,0:T(8,128)(2,1)S(1)}, bf16[192,896]{1,0:T(8,128)(2,1)}, u32[]{:S(2)}) copy-start(bf16[192,896]{1,0:T(8,128)(2,1)} %copy-done.4) | copy-start | bytes 1032196
